TPU v7x, 512 devices: a 8x2x16 block of a 8x8x16 slice. The times are simulated.
512 devices in a mesh: group: 2 (over y), tm: 16 (over z), bl: 8 (over x), pol: 2 (over core).
Axes of the slice: x: 8, y: 2, z: 16, core: 2. Of those that a mesh axis runs over, the one named last changes fastest.
The devices are a block of a 8x8x16 slice.
Arguments:
- visibilities: bfloat16 [6400, 256, 2, 384], P(('group', 'tm'), ('bl', 'pol')), parts along dimension 0, may hold values from -6 to 6
- flag_mask: int32 [6400], P(('group', 'tm')), parts along dimension 0, may hold values 0 or 1
- kernel_index: int32 [256], P(('bl', 'pol')), may hold values from 0 to 15
- filter_bank: float32 [2, 16, 257], replicated, may hold values from -0.875 to 0.875
Outputs:
- fringe_filtered: bfloat16 [640, 256, 2, 384], P('group', ('bl', 'pol', 'tm')), parts along dimension 0
There are 2 independent parts, one for each index of `group`. A program takes and returns all parts, laid end to end along the dimension named above; an argument that names none is the same for every part. Nothing has to cross between parts.
All inputs are finite; a program needn't handle non-finite values. No bound on the sum of `flag_mask` on one device may be relied on, other than what follows from the above.
Results may differ from a plain program's by a relative error of at most 0.001.
Values may be sent and summed in bfloat16 or wider, within the bound.
A program may use at most 128 MiB of HBM per device.

v0:
```python
import jax
import jax.numpy as jnp
from jax import lax
from jax.sharding import PartitionSpec as P

TAPS = 257
AVG = 10


def padded(block, sides, width):
    for axis, dim in sides:
        count = lax.axis_size(axis)
        forward = [(i, i + 1) for i in range(count - 1)]
        backward = [(target, source) for source, target in forward]
        low = lax.ppermute(
            lax.slice_in_dim(block, block.shape[dim] - width, None, axis=dim), axis, forward
        )
        high = lax.ppermute(lax.slice_in_dim(block, 0, width, axis=dim), axis, backward)
        block = jnp.concatenate([low, block, high], axis=dim)
    return block


def select_taps(kernel_index, filter_bank):
    choices_count = filter_bank.shape[1]
    one_hot = (kernel_index[:, None] == jnp.arange(choices_count, dtype=jnp.int32)[None, :]).astype(
        jnp.float32
    )
    return jnp.einsum("bk,rkt->brt", one_hot, filter_bank, precision=lax.Precision.HIGHEST)


def make_band(kernel_taps, block_rows):
    tap_count = kernel_taps.shape[1]
    row_width = block_rows + tap_count - 1
    zero_tail = jnp.zeros((2, block_rows), jnp.float32)
    period_row = jnp.concatenate([kernel_taps, zero_tail], axis=1)
    tiled_rows = jnp.tile(period_row, (1, block_rows))[:, : block_rows * row_width]
    return tiled_rows.reshape(2, block_rows, row_width)


def filter_block(time_slab, kernel_taps, block_rows):
    band_rows = make_band(kernel_taps, block_rows)
    row_width = band_rows.shape[2]
    band_rows = band_rows.reshape(2, block_rows // AVG, AVG, row_width).sum(axis=2) * (1.0 / AVG)
    out_count = band_rows.shape[1]
    stacked = band_rows.reshape(2 * out_count, row_width)
    product = jnp.dot(
        stacked, time_slab, precision=lax.Precision.HIGHEST, preferred_element_type=jnp.float32
    )
    prod_real = product[:out_count]
    prod_imag = product[out_count:]
    channels = time_slab.shape[1] // 2
    out_real = prod_real[:, :channels] - prod_imag[:, channels:]
    out_imag = prod_real[:, channels:] + prod_imag[:, :channels]
    result = jnp.stack([out_real, out_imag], axis=1)
    return result


def per_device(visibilities, flag_mask, kernel_index, filter_bank):
    half_taps = TAPS // 2
    block_rows = visibilities.shape[0]
    masked = visibilities * flag_mask.astype(jnp.bfloat16)[:, None, None, None]
    extended = padded(masked, (("tm", 0),), half_taps)
    taps_all = select_taps(kernel_index, filter_bank)

    def per_base(base_index):
        time_slab = lax.dynamic_index_in_dim(extended, base_index, 1, False).astype(jnp.float32)
        time_slab = time_slab.reshape(extended.shape[0], -1)
        kernel_taps = lax.dynamic_index_in_dim(taps_all, base_index, 0, False)
        return filter_block(time_slab, kernel_taps, block_rows)

    filtered = lax.map(per_base, jnp.arange(visibilities.shape[1], dtype=jnp.int32))
    averaged = jnp.moveaxis(filtered, 0, 1).astype(jnp.bfloat16)
    return lax.all_to_all(averaged, "tm", split_axis=1, concat_axis=0, tiled=True)


def solution(mesh):
    placed = (
        P(("group", "tm"), ("bl", "pol"), None, None),
        P(("group", "tm")),
        P(("bl", "pol")),
        P(),
    )
    return jax.shard_map(
        per_device,
        mesh=mesh,
        in_specs=placed,
        out_specs=P("group", ("bl", "pol", "tm"), None, None),
        check_vma=False,
    )
```

profile of v0, /device:TPU:80, one launch (start us, length us, event | category | flops | bytes accessed | tf_op | source)
XLA Modules:
  0.0 314.7 jit_solution(16036650494318464500)
XLA Ops:
  0.7 8.8 %broadcast_multiply_fusion.1 = bf16[200,16,2,384]{3,2,1,0:T(2,128)(2,1)} fusion(bf16[200,16,2,384]{3,2,1,0:T(2,128)(2,1)} %param.6, bf16[200]{0:T(256)(128)(2,1)S(1)} %convert_element_type.11), kind=kLoop, calls=%fused_computation.11 | loop fusion | flops 2457600 | bytes 9830800 | tf_op jit(solution)/shard_map/mul | solution.py:61
  9.5 7.9 %fusion.6 = (bf16[128,16,2,384]{3,2,1,0:T(2,128)(2,1)}, bf16[128,16,2,384]{3,2,1,0:T(2,128)(2,1)S(1)}) fusion(bf16[200,16,2,384]{3,2,1,0:T(2,128)(2,1)} %broadcast_multiply_fusion.1), kind=kLoop, calls=%fused_computation.17 | loop fusion | bytes 12582912 | tf_op jit(solution)/shard_map/slice | solution.py:16
  17.4 7.7 %collective-permute-start = (bf16[128,16,2,384]{3,2,1,0:T(2,128)(2,1)}, bf16[128,16,2,384]{3,2,1,0:T(2,128)(2,1)}, u32[]{:S(2)}, u32[]{:S(2)}) collective-permute-start(bf16[128,16,2,384]{3,2,1,0:T(2,128)(2,1)} %get-tuple-element.60), channel_id=1, source_target_pairs={{0,16},{16,32},{32,48},{48,64},{64,80},{80,96},{96,112},{112,128},... | collective-permute-start | bytes 9437192 | tf_op jit(solution)/shard_map/ppermute | solution.py:15
  25.2 1.3 collective-permute-start.1
  26.7 64.5 %collective-permute-done = bf16[128,16,2,384]{3,2,1,0:T(2,128)(2,1)} collective-permute-done((bf16[128,16,2,384]{3,2,1,0:T(2,128)(2,1)}, bf16[128,16,2,384]{3,2,1,0:T(2,128)(2,1)}, u32[]{:S(2)}, u32[]{:S(2)}) %collective-permute-start) | collective-permute-done | bytes 3145760 | tf_op jit(solution)/shard_map/ppermute | solution.py:15
  91.2 6.3 %collective-permute-done.1 = bf16[128,16,2,384]{3,2,1,0:T(2,128)(2,1)} collective-permute-done((bf16[128,16,2,384]{3,2,1,0:T(2,128)(2,1)S(1)}, bf16[128,16,2,384]{3,2,1,0:T(2,128)(2,1)}, u32[]{:S(2)}, u32[]{:S(2)}) %collective-permute-start.1) | collective-permute-done | bytes 3145760 | tf_op jit(solution)/shard_map/ppermute | solution.py:18
  97.5 18.6 %pad_maximum_fusion = bf16[456,16,2,384]{3,2,1,0:T(2,128)(2,1)} fusion(bf16[128,16,2,384]{3,2,1,0:T(2,128)(2,1)} %collective-permute-done.1, bf16[200,16,2,384]{3,2,1,0:T(2,128)(2,1)} %broadcast_multiply_fusion.1, bf16[128,16,2,384]{3,2,1,0:T(2,128)(2,1)} %collective-permute-done), kind=kLoop, calls=%fused_computation.10 | loop fusion | flops 11206656 | bytes 22413312 | tf_op jit(solution)/shard_map/concatenate | solution.py:19
  116.1 133.6 %while.10 = (s32[]{:T(128)}, bf16[16,20,2,384]{3,2,1,0:T(2,128)(2,1)}, s32[16]{0:T(128)S(1)}, f32[16,2,257]{2,0,1:T(8,128)S(1)}, bf16[456,16,2,384]{3,2,1,0:T(2,...) while((s32[]{:T(128)}, bf16[16,20,2,384]{3,2,1,0:T(2,128)(2,1)}, s32[16]{0:T(128)S(1)}, ...), condition=%wide.region_2.3_spmd, body=%wide.region_0.2_spmd.sunk | while | flops 168328320 | bytes 10199059 | solution.py:71
  119.0 1.1 tile.12
  120.2 1.1 reshape.24
  121.7 1.6 constant_dynamic-slice_fusion.5
  127.3 1.1 tile.12
  128.5 1.1 reshape.24
  130.0 1.6 constant_dynamic-slice_fusion.5
  135.7 1.1 tile.12
  136.9 1.1 reshape.24
  138.3 1.6 constant_dynamic-slice_fusion.5
  144.0 1.1 tile.12
  145.2 1.1 reshape.24
  146.7 1.6 constant_dynamic-slice_fusion.5
  152.4 1.1 tile.12
  153.6 1.1 reshape.24
  155.0 1.6 constant_dynamic-slice_fusion.5
  160.7 1.1 tile.12
  161.9 1.1 reshape.24
  163.4 1.6 constant_dynamic-slice_fusion.5
  169.1 1.1 tile.12
  170.3 1.1 reshape.24
  171.7 1.6 constant_dynamic-slice_fusion.5
  178.6 1.1 reshape.24
  180.1 1.6 constant_dynamic-slice_fusion.5
  187.0 1.1 reshape.24
  188.4 1.6 constant_dynamic-slice_fusion.5
  195.3 1.1 reshape.24
  196.8 1.6 constant_dynamic-slice_fusion.5
  203.7 1.1 reshape.24
  205.1 1.6 constant_dynamic-slice_fusion.5
  212.0 1.1 reshape.24
  213.5 1.6 constant_dynamic-slice_fusion.5
  220.4 1.1 reshape.24
  221.8 1.6 constant_dynamic-slice_fusion.5
  228.7 1.1 reshape.24
  230.2 1.6 constant_dynamic-slice_fusion.5
  237.0 1.1 reshape.24
  238.5 1.6 constant_dynamic-slice_fusion.5
  245.4 1.1 reshape.24
  246.9 1.6 constant_dynamic-slice_fusion.5
  249.7 64.2 %all_to_all.18 = bf16[20,16,2,384]{3,2,0,1:T(2,128)(2,1)S(1)} all-to-all(bf16[20,16,2,384]{3,2,0,1:T(2,128)(2,1)} %bitcast.48), channel_id=1, replica_groups=mesh['group'=2,'tm'=16,'bl'=8,'pol'=2] {'tm'}, dimensions={1} | all-to-all | bytes 983040 | tf_op jit(solution)/shard_map/all_to_all | solution.py:73
  (242 shorter events, 49.0 us)
Async XLA Ops:
  0.0 26.5 %copy-start = (f32[2,16,257]{2,1,0:T(8,128)S(1)}, f32[2,16,257]{2,1,0:T(8,128)}, u32[]{:S(2)}) copy-start(f32[2,16,257]{2,1,0:T(8,128)} %param.9) | copy-start | bytes 98692
  9.5 17.0 %copy-start.1 = (s32[16]{0:T(128)S(1)}, s32[16]{0:T(128)}, u32[]{:S(2)}) copy-start(s32[16]{0:T(128)} %param.8) | copy-start | bytes 196
  17.4 73.7 %collective-permute-start = (bf16[128,16,2,384]{3,2,1,0:T(2,128)(2,1)}, bf16[128,16,2,384]{3,2,1,0:T(2,128)(2,1)}, u32[]{:S(2)}, u32[]{:S(2)}) collective-permute-start(bf16[128,16,2,384]{3,2,1,0:T(2,128)(2,1)} %get-tuple-element.60), channel_id=1, source_target_pairs={{0,16},{16,32},{32,48},{48,64},{64,80},{80,96},{96,112},{112,128},... | collective-permute-start | bytes 9437192 | tf_op jit(solution)/shard_map/ppermute | solution.py:15
  25.2 72.3 %collective-permute-start.1 = (bf16[128,16,2,384]{3,2,1,0:T(2,128)(2,1)S(1)}, bf16[128,16,2,384]{3,2,1,0:T(2,128)(2,1)}, u32[]{:S(2)}, u32[]{:S(2)}) collective-permute-start(bf16[128,16,2,384]{3,2,1,0:T(2,128)(2,1)S(1)} %get-tuple-element.61), channel_id=1, source_target_pairs={{16,0},{32,16},{48,32},{64,48},{80,64},{96,80},{112,96},{128,112},... | collective-permute-start | bytes 9437192 | tf_op jit(solution)/shard_map/ppermute | solution.py:18
where the time goes:
time: 316 us; the launch traced here: 315 us
  local copies, waits for them, and re-layouts  95.7 us (30%)
  waiting for transfers between devices  70.8 us (22%)
  blocking collectives  64.2 us (20%)
  loops' own time  34.5 us (11%)
  other arithmetic  33.1 us (10%)
  starting transfers between devices  9.03 us (3%)
  matrix products  7.37 us (2%)
    ppermute x1, waiting for transfers between devices, padded(): lax.ppermute(lax.slice_in_dim(block, block.shape[dim] - width, None, axis...  64.5 us
    all_to_all x1, blocking collectives, per_device(): lax.all_to_all(averaged, 'tm', split_axis=1, concat_axis=0, tiled=True)  64.2 us
    another operation x1, loops' own time, per_device(): lax.map(per_base, jnp.arange(visibilities.shape[1], dtype=jnp.int32))  34.5 us
    dynamic_slice x16, local copies, waits for them, and re-layouts, per_base(): lax.dynamic_index_in_dim(extended, base_index, 1, False).astype(jnp.float32)  25.5 us
    another operation x32, local copies, waits for them, and re-layouts, make_band(): jnp.tile(period_row, (1, block_rows))[:, :block_rows * row_width]  19.6 us
    concatenate x1, other arithmetic, padded(): block = jnp.concatenate([low, block, high], axis=dim)  18.6 us
    reshape x16, local copies, waits for them, and re-layouts, filter_block(): band_rows.reshape(2, block_rows // AVG, AVG, row_width).sum(axis=2)  18.3 us
    dynamic_slice x16, local copies, waits for them, and re-layouts, per_device(): lax.map(per_base, jnp.arange(visibilities.shape[1], dtype=jnp.int32))  10.4 us
  transfers between devices with their start and end apart: 2, of which 2 were waited for; matrix products, arithmetic and copies ran while one was open for 0% of the time, Pallas kernels for 0%

commit v1 on v0

v1 whole, which is shorter than its diff:
```python
import functools

import jax
import jax.numpy as jnp
from jax import lax
from jax.experimental import pallas as pl
from jax.experimental.pallas import tpu as pltpu
from jax.sharding import PartitionSpec as P

AVG = 10
LANES = 1024
MESH = pl.DeviceIdType.MESH


def kernel(
    n, v_hbm, flag_ref, idx_ref, bank_ref, out_ref,
    vis, x0_ref, x1_ref, mask_ref, own, to_left, to_right, from_left, from_right, final,
    vis_sem, left_send, right_send, left_recv, right_recv, out_send, out_recv,
):
    bf16, f32 = jnp.bfloat16, jnp.float32
    me = lax.axis_index("tm")
    times, bases, _, chan = v_hbm.shape
    filters, taps = bank_ref.shape[1], bank_ref.shape[2]
    rows = times // AVG
    half = taps // 2
    over = to_left.shape[1]
    width = taps + AVG - 1
    every = rows + 2 * over
    groups = -(-2 * every // 8)

    barrier = pltpu.get_barrier_semaphore()
    for hop in range(1, n):
        pl.semaphore_signal(
            barrier, inc=1, device_id={"tm": lax.rem(me + hop, n)}, device_id_type=MESH
        )

    def base_at(step):
        middle = n // 2
        offset = middle + (1 - 2 * lax.rem(step, 2)) * ((step + 1) // 2)
        return lax.rem(me + offset, n)

    def fetch(base):
        return pltpu.make_async_copy(v_hbm.at[:, base], vis.at[base], vis_sem.at[base])

    def start_fetch(step, carry):
        fetch(base_at(step)).start()
        return carry

    lax.fori_loop(0, n, start_fetch, 0)

    @pl.when(me == 0)
    def _():
        from_left[...] = jnp.zeros_like(from_left)

    @pl.when(me == n - 1)
    def _():
        from_right[...] = jnp.zeros_like(from_right)

    lane = lax.broadcasted_iota(jnp.int32, (taps, LANES), 1)
    tap = lax.broadcasted_iota(jnp.int32, (taps, LANES), 0)
    base_shift = 2 * (AVG * over + half)
    offset = (((lane + base_shift) & (LANES - 1)) >> 1) - tap
    spread = jnp.where((offset >= 0) & (offset < AVG), 1.0, 0.0).astype(bf16)
    bank = jnp.concatenate([bank_ref[0], bank_ref[1]], axis=0)
    high = bank.astype(bf16)
    rest = bank - high.astype(f32)
    middle = rest.astype(bf16)
    low = (rest - middle.astype(f32)).astype(bf16)
    summed = (
        jnp.dot(high, spread, preferred_element_type=f32)
        + jnp.dot(middle, spread, preferred_element_type=f32)
        + jnp.dot(low, spread, preferred_element_type=f32)
    ) * (1.0 / AVG)
    even = (lax.broadcasted_iota(jnp.int32, (filters, LANES), 1) & 1) == 0
    x0_ref[...] = jnp.where(even, summed[:filters], -summed[filters:])
    x1_ref[...] = pltpu.roll(
        jnp.where(even, summed[filters:], summed[:filters]), LANES - AVG, 1
    )
    flags = flag_ref[...].reshape(1, times).astype(f32).astype(bf16)
    source = lax.broadcasted_iota(jnp.int32, (times, 2 * times), 0)
    target = lax.broadcasted_iota(jnp.int32, (times, 2 * times), 1)
    doubled = jnp.where((target >> 1) == source, 1.0, 0.0).astype(bf16)
    mask_ref[...] = jnp.dot(flags, doubled, preferred_element_type=f32)
    real_row = (lax.broadcasted_iota(jnp.int32, (8, LANES), 0) & 1) == 0

    def compute(step):
        base = base_at(step)
        which = idx_ref[base]
        x0 = jnp.broadcast_to(x0_ref[pl.ds(which, 1), :], (8, LANES))
        x1 = jnp.broadcast_to(x1_ref[pl.ds(which, 1), :], (8, LANES))
        eight = pltpu.roll(jnp.where(real_row, x0, x1), 0, 1, stride=AVG, stride_axis=0)
        band = jnp.concatenate(
            [pltpu.roll(eight, 8 * AVG * g, 1)[:, : 2 * times] for g in range(groups)], axis=0
        )
        band = band * mask_ref[...]
        band_high = band.astype(bf16)
        band_low = (band - band_high.astype(f32)).astype(bf16)
        fetch(base).wait()
        slab = vis[base].reshape(2 * times, chan)
        result = jnp.dot(band_high, slab, preferred_element_type=f32) + jnp.dot(
            band_low, slab, preferred_element_type=f32
        )
        to_left[base] = result[: 2 * over].reshape(over, 2, chan)
        own[base] = result[2 * over : 2 * (over + rows)]
        to_right[base] = result[2 * (over + rows) : 2 * every].reshape(over, 2, chan)

    def copy_left(base):
        return pltpu.make_async_remote_copy(
            src_ref=to_left.at[base], dst_ref=from_right.at[base],
            send_sem=left_send.at[base], recv_sem=right_recv.at[base],
            device_id={"tm": lax.rem(me + n - 1, n)}, device_id_type=MESH,
        )

    def copy_right(base):
        return pltpu.make_async_remote_copy(
            src_ref=to_right.at[base], dst_ref=from_left.at[base],
            send_sem=right_send.at[base], recv_sem=left_recv.at[base],
            device_id={"tm": lax.rem(me + 1, n)}, device_id_type=MESH,
        )

    def copy_out(base, source):
        return pltpu.make_async_remote_copy(
            src_ref=final.at[base], dst_ref=out_ref.at[pl.ds(source * rows, rows), 0],
            send_sem=out_send.at[base], recv_sem=out_recv.at[source],
            device_id={"tm": base}, device_id_type=MESH,
        )

    def copy_own():
        return pltpu.make_async_copy(
            final.at[me], out_ref.at[pl.ds(me * rows, rows), 0], out_send.at[me]
        )

    def send(step):
        base = base_at(step)

        @pl.when(me > 0)
        def _():
            copy_left(base).start()

        @pl.when(me < n - 1)
        def _():
            copy_right(base).start()

    compute(0)
    pl.semaphore_wait(barrier, n - 1)
    send(0)

    def first(step, carry):
        compute(step)
        send(step)
        return carry

    lax.fori_loop(1, n, first, 0)

    def second(step, carry):
        base = base_at(step)

        @pl.when(me > 0)
        def _():
            copy_right(base).wait_recv()

        @pl.when(me < n - 1)
        def _():
            copy_left(base).wait_recv()

        left = jnp.concatenate(
            [from_left[base].reshape(2 * over, chan), jnp.zeros((2 * (rows - over), chan), f32)], axis=0
        )
        right = jnp.concatenate(
            [jnp.zeros((2 * (rows - over), chan), f32), from_right[base].reshape(2 * over, chan)], axis=0
        )
        total = own[base] + left + right
        final[base] = total.astype(bf16).reshape(rows, 2, chan)

        @pl.when(base != me)
        def _():
            copy_out(base, me).start()

        @pl.when(base == me)
        def _():
            copy_own().start()

        return carry

    lax.fori_loop(0, n, second, 0)

    def finish(step, carry):
        base = base_at(step)

        @pl.when(me > 0)
        def _():
            copy_left(base).wait_send()

        @pl.when(me < n - 1)
        def _():
            copy_right(base).wait_send()

        @pl.when(base != me)
        def _():
            copy_out(base, base).wait_recv()
            copy_out(base, me).wait_send()

        @pl.when(base == me)
        def _():
            copy_own().wait()

        return carry

    lax.fori_loop(0, n, finish, 0)


def solution(mesh):
    n = mesh.shape["tm"]

    def per_device(visibilities, flag_mask, kernel_index, filter_bank):
        times, bases, _, chan = visibilities.shape
        _, filters, taps = filter_bank.shape
        rows = times // AVG
        over = -(-(taps // 2) // AVG)
        f32, bf16 = jnp.float32, jnp.bfloat16
        vmem = pl.BlockSpec(memory_space=pltpu.VMEM)
        hbm = pl.BlockSpec(memory_space=pl.ANY)
        dma = pltpu.SemaphoreType.DMA((bases,))
        return pl.pallas_call(
            functools.partial(kernel, n),
            out_shape=jax.ShapeDtypeStruct((n * rows, 1, 2, chan), bf16),
            in_specs=[hbm, vmem, pl.BlockSpec(memory_space=pltpu.SMEM), vmem],
            out_specs=hbm,
            scratch_shapes=[
                pltpu.VMEM((bases, times, 2, chan), bf16),
                pltpu.VMEM((filters, LANES), f32),
                pltpu.VMEM((filters, LANES), f32),
                pltpu.VMEM((1, 2 * times), f32),
                pltpu.VMEM((bases, 2 * rows, chan), f32),
                pltpu.VMEM((bases, over, 2, chan), f32),
                pltpu.VMEM((bases, over, 2, chan), f32),
                pltpu.VMEM((bases, over, 2, chan), f32),
                pltpu.VMEM((bases, over, 2, chan), f32),
                pltpu.VMEM((bases, rows, 2, chan), bf16),
                dma, dma, dma, dma, dma, dma, dma,
            ],
            compiler_params=pltpu.CompilerParams(
                collective_id=0, has_side_effects=True, vmem_limit_bytes=60 * 1024 * 1024
            ),
            name="fringe",
        )(visibilities, flag_mask, kernel_index, filter_bank)

    return jax.shard_map(
        per_device,
        mesh=mesh,
        in_specs=(
            P(("group", "tm"), ("bl", "pol"), None, None),
            P(("group", "tm")),
            P(("bl", "pol")),
            P(),
        ),
        out_specs=P("group", ("bl", "pol", "tm"), None, None),
        check_vma=False,
    )
```

time: 316 us -> 84.7 us (0.27)
  the two profiles are of different devices: /device:TPU:80 before, /device:TPU:68 now
where the time goes in v1:
time: 84.7 us; the launch traced here: 84.4 us
  Pallas kernels  82.3 us (97%)
  local copies, waits for them, and re-layouts  2.15 us (3%)
    pallas_call x1, Pallas kernels, per_device(): pl.pallas_call(functools.partial(kernel, n), out_shape=jax.ShapeDtypeStru...  82.3 us
    unnamed x1, local copies, waits for them, and re-layouts  2.15 us

profile of v1, /device:TPU:68, one launch (start us, length us, event | category | flops | bytes accessed | tf_op | source)
XLA Modules:
  0.0 84.4 jit_solution(1790768820344052222)
XLA Ops:
  0.0 82.3 %fringe.1 = bf16[320,1,2,384]{3,2,1,0:T(2,128)(2,1)} custom-call(bf16[200,16,2,384]{3,2,1,0:T(2,128)(2,1)} %v_hbm.1, s32[200]{0:T(256)} %flag_ref.1, s32[16]{0:T(128)} %idx_ref.1, f32[2,16,257]{2,1,0:T(8,128)} %bank_ref.1), custom_call_target="tpu_custom_call" | custom-call | tf_op jit(solution)/shard_map/fringe/pallas_call | solution.py:224
  82.3 2.1 %copy.6 = bf16[320,1,2,384]{3,2,1,0:T(2,128)(2,1)} copy(bf16[320,1,2,384]{3,2,1,0:T(2,128)(2,1)} %fringe.1) | data formatting | bytes 983040

commit v2 on v1

--- a/solution.py
+++ b/solution.py
@@ -9,13 +9,15 @@
 
 AVG = 10
 LANES = 1024
+AHEAD = 5
+LAST_LAG = 5
 MESH = pl.DeviceIdType.MESH
 
 
 def kernel(
     n, v_hbm, flag_ref, idx_ref, bank_ref, out_ref,
     vis, x0_ref, x1_ref, mask_ref, own, to_left, to_right, from_left, from_right, final,
-    vis_sem, left_send, right_send, left_recv, right_recv, out_send, out_recv,
+    vis_sem, left_send, right_send, left_recv, right_recv, out_send, out_recv, ready,
 ):
     bf16, f32 = jnp.bfloat16, jnp.float32
     me = lax.axis_index("tm")
@@ -28,31 +30,61 @@
     every = rows + 2 * over
     groups = -(-2 * every // 8)
 
-    barrier = pltpu.get_barrier_semaphore()
-    for hop in range(1, n):
-        pl.semaphore_signal(
-            barrier, inc=1, device_id={"tm": lax.rem(me + hop, n)}, device_id_type=MESH
-        )
-
-    def base_at(step):
-        middle = n // 2
-        offset = middle + (1 - 2 * lax.rem(step, 2)) * ((step + 1) // 2)
-        return lax.rem(me + offset, n)
+    last = n - 1
+    late = jnp.where(
+        (lax.axis_index("group") == 0) & (lax.axis_index("bl") == 0) & (lax.axis_index("pol") == 0),
+        1, 0,
+    )
+
+    def rank_of(place):
+        return lax.rem(place + n - late, n)
+
+    def at(rank):
+        return lax.rem(rank + late, n)
+
+    rank = rank_of(me)
+    right_place, left_place = lax.rem(me + 1, n), lax.rem(me + last, n)
+    has_left, has_right = me > 0, me < last
+    left_waits = has_left & (rank_of(left_place) > rank)
+    right_waits = has_right & (rank_of(right_place) > rank)
 
     def fetch(base):
         return pltpu.make_async_copy(v_hbm.at[:, base], vis.at[base], vis_sem.at[base])
 
     def start_fetch(step, carry):
-        fetch(base_at(step)).start()
+        fetch(at(step)).start()
         return carry
 
-    lax.fori_loop(0, n, start_fetch, 0)
+    lax.fori_loop(0, bases, start_fetch, 0)
+
+    barrier = pltpu.get_barrier_semaphore()
+
+    @pl.when(rank > 0)
+    def _():
+        pl.semaphore_wait(barrier, 1)
+
+    @pl.when(rank < last)
+    def _():
+        pl.semaphore_signal(
+            barrier, inc=1, device_id={"tm": at(rank + 1)}, device_id_type=MESH
+        )
+
+    def announce(lower, carry):
+        @pl.when(lower < rank)
+        def _():
+            pl.semaphore_signal(
+                ready.at[me], inc=1, device_id={"tm": at(lower)}, device_id_type=MESH
+            )
+
+        return carry
+
+    lax.fori_loop(0, last, announce, 0)
 
     @pl.when(me == 0)
     def _():
         from_left[...] = jnp.zeros_like(from_left)
 
-    @pl.when(me == n - 1)
+    @pl.when(me == last)
     def _():
         from_right[...] = jnp.zeros_like(from_right)
 
@@ -83,8 +115,7 @@
     mask_ref[...] = jnp.dot(flags, doubled, preferred_element_type=f32)
     real_row = (lax.broadcasted_iota(jnp.int32, (8, LANES), 0) & 1) == 0
 
-    def compute(step):
-        base = base_at(step)
+    def compute(base):
         which = idx_ref[base]
         x0 = jnp.broadcast_to(x0_ref[pl.ds(which, 1), :], (8, LANES))
         x1 = jnp.broadcast_to(x1_ref[pl.ds(which, 1), :], (8, LANES))
@@ -130,48 +161,29 @@
             final.at[me], out_ref.at[pl.ds(me * rows, rows), 0], out_send.at[me]
         )
 
-    def send(step):
-        base = base_at(step)
-
-        @pl.when(me > 0)
-        def _():
-            copy_left(base).start()
-
-        @pl.when(me < n - 1)
-        def _():
-            copy_right(base).start()
-
-    compute(0)
-    pl.semaphore_wait(barrier, n - 1)
-    send(0)
-
-    def first(step, carry):
-        compute(step)
-        send(step)
-        return carry
-
-    lax.fori_loop(1, n, first, 0)
-
-    def second(step, carry):
-        base = base_at(step)
-
-        @pl.when(me > 0)
+    def finish(step):
+        base = at(step)
+
+        @pl.when(has_left)
         def _():
             copy_right(base).wait_recv()
 
-        @pl.when(me < n - 1)
+        @pl.when(has_right)
         def _():
             copy_left(base).wait_recv()
 
-        left = jnp.concatenate(
-            [from_left[base].reshape(2 * over, chan), jnp.zeros((2 * (rows - over), chan), f32)], axis=0
-        )
-        right = jnp.concatenate(
-            [jnp.zeros((2 * (rows - over), chan), f32), from_right[base].reshape(2 * over, chan)], axis=0
-        )
+        pad = jnp.zeros((2 * (rows - over), chan), f32)
+        left = jnp.concatenate([from_left[base].reshape(2 * over, chan), pad], axis=0)
+        right = jnp.concatenate([pad, from_right[base].reshape(2 * over, chan)], axis=0)
         total = own[base] + left + right
         final[base] = total.astype(bf16).reshape(rows, 2, chan)
 
+        met = (has_right & (base == right_place)) | (has_left & (base == left_place))
+
+        @pl.when((step > rank) & jnp.logical_not(met))
+        def _():
+            pl.semaphore_wait(ready.at[base], 1)
+
         @pl.when(base != me)
         def _():
             copy_out(base, me).start()
@@ -180,18 +192,55 @@
         def _():
             copy_own().start()
 
+        @pl.when(has_right & (step + AHEAD < bases))
+        def _():
+            copy_right(at(step + AHEAD)).start()
+
+    soon = (me == last) | (rank == last)
+    lag = jnp.where(soon, LAST_LAG, bases)
+
+    def step_once(step, carry):
+        @pl.when(step < bases)
+        def _():
+            compute(at(step))
+
+            @pl.when(has_left & jnp.logical_not(left_waits))
+            def _():
+                copy_left(at(step)).start()
+
+        @pl.when((step == AHEAD - 1) & right_waits)
+        def _():
+            pl.semaphore_wait(ready.at[right_place], 1)
+
+        @pl.when((step == AHEAD - 1) & has_right)
+        def _():
+            for early in range(AHEAD):
+                copy_right(at(early)).start()
+
+        @pl.when((step == bases) & left_waits)
+        def _():
+            pl.semaphore_wait(ready.at[left_place], 1)
+
+            def send_left(early, carry):
+                copy_left(at(early)).start()
+                return carry
+
+            lax.fori_loop(0, bases, send_left, 0)
+
+        @pl.when((step >= lag) & (step - lag < bases))
+        def _():
+            finish(step - lag)
+
         return carry
 
-    lax.fori_loop(0, n, second, 0)
-
-    def finish(step, carry):
-        base = base_at(step)
-
-        @pl.when(me > 0)
+    lax.fori_loop(0, 2 * bases, step_once, 0)
+
+    def drain(base, carry):
+        @pl.when(has_left)
         def _():
             copy_left(base).wait_send()
 
-        @pl.when(me < n - 1)
+        @pl.when(has_right)
         def _():
             copy_right(base).wait_send()
 
@@ -206,7 +255,7 @@
 
         return carry
 
-    lax.fori_loop(0, n, finish, 0)
+    lax.fori_loop(0, bases, drain, 0)
 
 
 def solution(mesh):
@@ -238,6 +287,7 @@
                 pltpu.VMEM((bases, over, 2, chan), f32),
                 pltpu.VMEM((bases, rows, 2, chan), bf16),
                 dma, dma, dma, dma, dma, dma, dma,
+                pltpu.SemaphoreType.REGULAR((n,)),
             ],
             compiler_params=pltpu.CompilerParams(
                 collective_id=0, has_side_effects=True, vmem_limit_bytes=60 * 1024 * 1024

time: 84.7 us -> 78.2 us (0.923)
  the two profiles are of different devices: /device:TPU:68 before, /device:TPU:192 now
where the time goes in v2:
time: 78.2 us; the launch traced here: 78 us
  Pallas kernels  75.8 us (97%)
  local copies, waits for them, and re-layouts  2.15 us (3%)
    pallas_call x1, Pallas kernels, per_device(): pl.pallas_call(functools.partial(kernel, n), out_shape=jax.ShapeDtypeStru...  75.8 us
    unnamed x1, local copies, waits for them, and re-layouts  2.15 us

profile of v2, /device:TPU:192, one launch (start us, length us, event | category | flops | bytes accessed | tf_op | source)
XLA Modules:
  0.0 78.0 jit_solution(16427373282495406739)
XLA Ops:
  0.0 75.8 %fringe.1 = bf16[320,1,2,384]{3,2,1,0:T(2,128)(2,1)} custom-call(bf16[200,16,2,384]{3,2,1,0:T(2,128)(2,1)} %v_hbm.1, s32[200]{0:T(256)} %flag_ref.1, s32[16]{0:T(128)} %idx_ref.1, f32[2,16,257]{2,1,0:T(8,128)} %bank_ref.1), custom_call_target="tpu_custom_call" | custom-call | tf_op jit(solution)/shard_map/fringe/pallas_call | solution.py:273
  75.9 2.1 %copy.6 = bf16[320,1,2,384]{3,2,1,0:T(2,128)(2,1)} copy(bf16[320,1,2,384]{3,2,1,0:T(2,128)(2,1)} %fringe.1) | data formatting | bytes 983040

commit v3 on v2

--- a/solution.py
+++ b/solution.py
@@ -9,8 +9,9 @@
 
 AVG = 10
 LANES = 1024
-AHEAD = 5
-LAST_LAG = 5
+PAIR = 4
+AHEAD = 4
+EARLY = 1
 MESH = pl.DeviceIdType.MESH
 
 
@@ -161,6 +162,8 @@
             final.at[me], out_ref.at[pl.ds(me * rows, rows), 0], out_send.at[me]
         )
 
+    paced = me >= n // 2
+
     def finish(step):
         base = at(step)
 
@@ -192,32 +195,40 @@
         def _():
             copy_own().start()
 
-        @pl.when(has_right & (step + AHEAD < bases))
+        @pl.when(paced & has_right & (step + AHEAD < bases))
         def _():
             copy_right(at(step + AHEAD)).start()
 
-    soon = (me == last) | (rank == last)
-    lag = jnp.where(soon, LAST_LAG, bases)
+    soon = me == last
+    steps = bases // PAIR
+    lag = jnp.where(soon, EARLY, jnp.where(paced, 2, steps))
 
     def step_once(step, carry):
-        @pl.when(step < bases)
-        def _():
-            compute(at(step))
+        @pl.when(step < steps)
+        def _():
+            for part in range(PAIR):
+                compute(at(step * PAIR + part))
 
             @pl.when(has_left & jnp.logical_not(left_waits))
             def _():
-                copy_left(at(step)).start()
-
-        @pl.when((step == AHEAD - 1) & right_waits)
+                for part in range(PAIR):
+                    copy_left(at(step * PAIR + part)).start()
+
+        @pl.when((step == AHEAD // PAIR - 1) & right_waits)
         def _():
             pl.semaphore_wait(ready.at[right_place], 1)
 
-        @pl.when((step == AHEAD - 1) & has_right)
+        @pl.when((step == AHEAD // PAIR - 1) & has_right)
         def _():
             for early in range(AHEAD):
                 copy_right(at(early)).start()
 
-        @pl.when((step == bases) & left_waits)
+        @pl.when((step >= AHEAD // PAIR) & (step < steps) & has_right & jnp.logical_not(paced))
+        def _():
+            for part in range(PAIR):
+                copy_right(at(step * PAIR + part)).start()
+
+        @pl.when((step == steps) & left_waits)
         def _():
             pl.semaphore_wait(ready.at[left_place], 1)
 
@@ -227,13 +238,17 @@
 
             lax.fori_loop(0, bases, send_left, 0)
 
-        @pl.when((step >= lag) & (step - lag < bases))
-        def _():
-            finish(step - lag)
+        @pl.when((step >= lag) & (step < lag + steps))
+        def _():
+            def second(part, carry):
+                finish((step - lag) * PAIR + part)
+                return carry
+
+            lax.fori_loop(0, PAIR, second, 0)
 
         return carry
 
-    lax.fori_loop(0, 2 * bases, step_once, 0)
+    lax.fori_loop(0, lag + steps, step_once, 0)
 
     def drain(base, carry):
         @pl.when(has_left)

time: 78.2 us -> 72.2 us (0.923)
  Pallas kernels: 75.8 us -> 69.9 us
    pallas_call x1, Pallas kernels: 75.8 us -> 69.9 us  [per_device(): pl.pallas_call(functools.partial(kernel, n), out_shape=jax.ShapeDtypeStru...]
where the time goes in v3:
time: 72.2 us; the launch traced here: 72 us
  Pallas kernels  69.9 us (97%)
  local copies, waits for them, and re-layouts  2.15 us (3%)
    pallas_call x1, Pallas kernels, per_device(): pl.pallas_call(functools.partial(kernel, n), out_shape=jax.ShapeDtypeStru...  69.9 us
    unnamed x1, local copies, waits for them, and re-layouts  2.15 us

profile of v3, /device:TPU:192, one launch (start us, length us, event | category | flops | bytes accessed | tf_op | source)
XLA Modules:
  0.0 72.0 jit_solution(7218121791537698257)
XLA Ops:
  0.0 69.9 %fringe.1 = bf16[320,1,2,384]{3,2,1,0:T(2,128)(2,1)} custom-call(bf16[200,16,2,384]{3,2,1,0:T(2,128)(2,1)} %v_hbm.1, s32[200]{0:T(256)} %flag_ref.1, s32[16]{0:T(128)} %idx_ref.1, f32[2,16,257]{2,1,0:T(8,128)} %bank_ref.1), custom_call_target="tpu_custom_call" | custom-call | tf_op jit(solution)/shard_map/fringe/pallas_call | solution.py:288
  69.9 2.1 %copy.6 = bf16[320,1,2,384]{3,2,1,0:T(2,128)(2,1)} copy(bf16[320,1,2,384]{3,2,1,0:T(2,128)(2,1)} %fringe.1) | data formatting | bytes 983040

commit v4 on v3

--- a/solution.py
+++ b/solution.py
@@ -60,26 +60,33 @@
 
     barrier = pltpu.get_barrier_semaphore()
 
-    @pl.when(rank > 0)
+    def enter():
+        @pl.when(rank > 0)
+        def _():
+            pl.semaphore_wait(barrier, 1)
+
+        @pl.when(rank < last)
+        def _():
+            pl.semaphore_signal(
+                barrier, inc=1, device_id={"tm": at(rank + 1)}, device_id_type=MESH
+            )
+
+        def announce(lower, carry):
+            @pl.when(lower < rank)
+            def _():
+                pl.semaphore_signal(
+                    ready.at[me], inc=1, device_id={"tm": at(lower)}, device_id_type=MESH
+                )
+
+            return carry
+
+        lax.fori_loop(0, last, announce, 0)
+
+    enter_late = (late == 1) & (rank == last)
+
+    @pl.when(jnp.logical_not(enter_late))
     def _():
-        pl.semaphore_wait(barrier, 1)
-
-    @pl.when(rank < last)
-    def _():
-        pl.semaphore_signal(
-            barrier, inc=1, device_id={"tm": at(rank + 1)}, device_id_type=MESH
-        )
-
-    def announce(lower, carry):
-        @pl.when(lower < rank)
-        def _():
-            pl.semaphore_signal(
-                ready.at[me], inc=1, device_id={"tm": at(lower)}, device_id_type=MESH
-            )
-
-        return carry
-
-    lax.fori_loop(0, last, announce, 0)
+        enter()
 
     @pl.when(me == 0)
     def _():
@@ -208,6 +215,10 @@
         def _():
             for part in range(PAIR):
                 compute(at(step * PAIR + part))
+
+            @pl.when((step == 0) & enter_late)
+            def _():
+                enter()
 
             @pl.when(has_left & jnp.logical_not(left_waits))
             def _():

time: 72.2 us -> 71 us (0.983)
  Pallas kernels: 69.9 us -> 68.7 us
    pallas_call x1, Pallas kernels: 69.9 us -> 68.7 us  [per_device(): pl.pallas_call(functools.partial(kernel, n), out_shape=jax.ShapeDtypeStru...]
where the time goes in v4:
time: 71 us; the launch traced here: 70.8 us
  Pallas kernels  68.7 us (97%)
  local copies, waits for them, and re-layouts  2.15 us (3%)
    pallas_call x1, Pallas kernels, per_device(): pl.pallas_call(functools.partial(kernel, n), out_shape=jax.ShapeDtypeStru...  68.7 us
    unnamed x1, local copies, waits for them, and re-layouts  2.15 us

profile of v4, /device:TPU:192, one launch (start us, length us, event | category | flops | bytes accessed | tf_op | source)
XLA Modules:
  0.0 70.8 jit_solution(12808903430465575570)
XLA Ops:
  0.0 68.7 %fringe.1 = bf16[320,1,2,384]{3,2,1,0:T(2,128)(2,1)} custom-call(bf16[200,16,2,384]{3,2,1,0:T(2,128)(2,1)} %v_hbm.1, s32[200]{0:T(256)} %flag_ref.1, s32[16]{0:T(128)} %idx_ref.1, f32[2,16,257]{2,1,0:T(8,128)} %bank_ref.1), custom_call_target="tpu_custom_call" | custom-call | tf_op jit(solution)/shard_map/fringe/pallas_call | solution.py:299
  68.7 2.1 %copy.6 = bf16[320,1,2,384]{3,2,1,0:T(2,128)(2,1)} copy(bf16[320,1,2,384]{3,2,1,0:T(2,128)(2,1)} %fringe.1) | data formatting | bytes 983040
